TPU v7x, 32 devices: a whole 2x2x4 slice. The times are simulated.
32 devices in a mesh: dp: 16 (over z, y, core), tensor: 2 (over x).
Axes of the slice: x: 2, y: 2, z: 4, core: 2. Of those that a mesh axis runs over, the one named last changes fastest.
Arguments:
- token_ids: int32 [8192], P('dp'), may hold values from 0 to 30719
- lengths: int32 [16], P('dp'), may hold values from 128 to 512
- word_table: bfloat16 [30720, 1024], P('tensor'), may hold values from -6 to 6
- pos_table: bfloat16 [512, 1024], replicated, may hold values from -4 to 4
- w_qkv: bfloat16 [2, 3, 1024, 1024], P(None, None, 'dp', 'tensor'), may hold values from -0.1875 to 0.1875
- w_out: bfloat16 [2, 1024, 1024], P(None, 'dp', 'tensor'), may hold values from -0.1875 to 0.1875
- w_up: bfloat16 [2, 1024, 4096], P(None, 'dp', 'tensor'), may hold values from -0.1875 to 0.1875
- w_down: bfloat16 [2, 1024, 4096], P(None, 'dp', 'tensor'), may hold values from -0.09375 to 0.09375
- up_bias: float32 [2, 4096], P(None, 'tensor'), may hold values from -3 to 3
- dense_bias: float32 [2, 2, 1024], replicated, may hold values from -3 to 3
- norm_gain: float32 [5, 1024], replicated, may hold values from 0.1 to 1.9
- norm_bias: float32 [5, 1024], replicated, may hold values from -3 to 3
Outputs:
- encoded: bfloat16 [8192, 1024], P('dp', 'tensor')
- similarity: float32 [16, 16], P('dp')
All inputs are finite; a program needn't handle non-finite values.
Results may differ from a plain program's by a relative error of at most 0.015.
Values may be sent and summed in bfloat16 or wider, within the bound.
A program may use at most 128 MiB of HBM per device.

v0:
```python
import jax
import jax.numpy as jnp
from jax import lax
from jax.sharding import PartitionSpec as P

D = 1024
BLOCK = 512
LAYERS = 2
HEAD = 64
EPS = 1e-05


def layer_norm(values, gain, shift):
    average = jnp.mean(values, axis=-1, keepdims=True)
    centered = values - average
    spread = jnp.mean(centered * centered, axis=-1, keepdims=True)
    return centered * lax.rsqrt(spread + EPS) * gain + shift


def settle(partial_value, residual, bias_row, gain, shift, which):
    if which == 0:
        summed = lax.psum(partial_value, "tensor").astype(jnp.float32)
    else:
        summed = lax.psum(partial_value, "tensor").astype(jnp.float32)
    return layer_norm(residual.astype(jnp.float32) + summed + bias_row, gain, shift).astype(
        jnp.bfloat16
    )


def project_back(left, weight):
    product = lax.dot_general(
        left, weight, (((1,), (1,)), ((), ())), preferred_element_type=jnp.float32
    )
    return product.astype(jnp.bfloat16)


def per_device(
    token_ids,
    lengths,
    word_table,
    pos_table,
    w_qkv,
    w_out,
    w_up,
    w_down,
    up_bias,
    dense_bias,
    norm_gain,
    norm_bias,
):
    passage_count = lengths.shape[0]
    vocab_rows = word_table.shape[0]
    local_ids = token_ids - lax.axis_index("tensor") * vocab_rows
    inside = (local_ids >= 0) & (local_ids < vocab_rows)
    picked = jnp.take(word_table, jnp.clip(local_ids, 0, vocab_rows - 1), axis=0)
    picked = jnp.where(inside[:, None], picked, jnp.zeros_like(picked))
    embedded = lax.psum(picked, "tensor").astype(jnp.float32)
    embedded = embedded.reshape(passage_count, BLOCK, D) + pos_table.astype(jnp.float32)[None]
    hidden = layer_norm(
        embedded.reshape(passage_count * BLOCK, D), norm_gain[0], norm_bias[0]
    ).astype(jnp.bfloat16)
    visible = jnp.arange(BLOCK, dtype=jnp.int32)[None, :] < lengths[:, None]
    local_heads = w_qkv.shape[3] // HEAD
    scale_dot = 1.0 / jnp.sqrt(jnp.float32(HEAD))
    for layer in range(LAYERS):
        columns = hidden
        projected = jnp.einsum(
            "td,idc->itc",
            columns,
            lax.all_gather(w_qkv[layer], "dp", axis=1, tiled=True),
            preferred_element_type=jnp.float32,
        )
        projected = projected.astype(jnp.bfloat16).reshape(
            3, passage_count, BLOCK, local_heads, HEAD
        )
        scores = (
            jnp.einsum(
                "cqhe,ckhe->chqk", projected[0], projected[1], preferred_element_type=jnp.float32
            )
            * scale_dot
        )
        scores = jnp.where(visible[:, None, None, :], scores, jnp.float32(-1e30))
        top = jnp.max(scores, axis=-1, keepdims=True)
        expo = jnp.exp(scores - top)
        weights_soft = (expo / jnp.sum(expo, axis=-1, keepdims=True)).astype(jnp.bfloat16)
        context = jnp.einsum(
            "chqk,ckhe->cqhe", weights_soft, projected[2], preferred_element_type=jnp.float32
        )
        context = context.astype(jnp.bfloat16).reshape(passage_count * BLOCK, local_heads * HEAD)
        attended = project_back(context, lax.all_gather(w_out[layer], "dp", axis=0, tiled=True))
        middle = settle(
            attended,
            hidden,
            dense_bias[layer, 0],
            norm_gain[2 * layer + 1],
            norm_bias[2 * layer + 1],
            0,
        )
        raised = jnp.dot(
            middle,
            lax.all_gather(w_up[layer], "dp", axis=0, tiled=True),
            preferred_element_type=jnp.float32,
        )
        inner = jax.nn.gelu(raised + up_bias[layer], approximate=False).astype(jnp.bfloat16)
        mlp_out = project_back(inner, lax.all_gather(w_down[layer], "dp", axis=0, tiled=True))
        hidden = settle(
            mlp_out,
            middle,
            dense_bias[layer, 1],
            norm_gain[2 * layer + 2],
            norm_bias[2 * layer + 2],
            1,
        )
    width_share = hidden.shape[1] // lax.axis_size("tensor")
    encoded = lax.dynamic_slice_in_dim(
        hidden, lax.axis_index("tensor") * width_share, width_share, 1
    )
    weights_pool = visible.astype(jnp.float32)
    states = hidden.reshape(passage_count, BLOCK, D).astype(jnp.float32)
    pooled = (
        jnp.sum(weights_pool[:, :, None] * states, axis=1) / lengths.astype(jnp.float32)[:, None]
    )
    unit = pooled * lax.rsqrt(jnp.sum(pooled * pooled, axis=1, keepdims=True) + 1e-06)
    every_unit = lax.all_gather(unit, "dp", axis=0, tiled=True)
    similarity = jnp.dot(
        unit, every_unit.T, precision=lax.Precision.HIGHEST, preferred_element_type=jnp.float32
    )
    return (encoded, similarity)


def solution(mesh):
    in_specs = (
        P("dp"),
        P("dp"),
        P("tensor", None),
        P(),
        P(None, None, "dp", "tensor"),
        P(None, "dp", "tensor"),
        P(None, "dp", "tensor"),
        P(None, "dp", "tensor"),
        P(None, "tensor"),
        P(),
        P(),
        P(),
    )
    out_specs = (P("dp", "tensor"), P("dp", None))
    return jax.shard_map(
        per_device, mesh=mesh, in_specs=in_specs, out_specs=out_specs, check_vma=False
    )
```

profile of v0, /device:TPU:0, one launch (start us, length us, event | category | flops | bytes accessed | tf_op | source)
XLA Modules:
  0.0 518.2 jit_solution(6977902281912645279)
XLA Ops:
  8.0 0.7 compare_and_fusion
  8.8 12.5 %gather_fusion = bf16[512,1024]{1,0:T(8,128)(2,1)S(1)} fusion(bf16[15360,1024]{1,0:T(8,128)(2,1)} %param.14, s32[1024]{0:T(1024)S(1)} %pad_clamp_fusion), kind=kCustom, calls=%fused_computation | custom fusion | bytes 2099200 | tf_op jit(solution)/shard_map/jit(_take)/gather | solution.py:55
  21.3 1.2 select_select_fusion
  22.6 0.8 fusion.159
  23.5 0.7 fusion.160
  24.9 40.1 %all-reduce.6.cloned.1.call-done = bf16[512,1024]{1,0:T(8,128)(2,1)} async-done(((bf16[512,1024]{1,0:T(8,128)(2,1)}), bf16[512,1024]{1,0:T(8,128)(2,1)}) %all-reduce.6.cloned.1.call-update) | async-done | bytes 1048592 | tf_op jit(solution)/shard_map/psum | solution.py:57
  65.1 1.7 fusion.49
  66.7 1.7 multiply_reduce_fusion.5
  69.0 4.2 all-gather.18.cloned.1.call-done
  73.2 3.7 fusion.67
  77.1 5.3 %fusion.165 = (f32[8,512]{1,0:T(8,128)S(1)}, f32[8,512,512]{1,2,0:T(8,128)}) fusion(pred[512]{0:T(512)(128)(4,1)S(1)} %iota_compare_fusion, bf16[512,8,64]{0,2,1:T(8,128)(2,1)S(1)} %bitcast.119, bf16[512,8,64]{0,2,1:T(8,128)(2,1)S(1)} %bitcast.118), kind=kOutput, calls=%fused_computation.202 | convolution fusion | flops 276824576 | bytes 9454080 | tf_op jit(solution)/shard_map/sub | solution.py:84
  82.4 4.2 fusion.81
  86.7 24.9 %all-gather.20.cloned.1.call-done = bf16[1,1024,512]{2,1,0:T(8,128)(2,1)} async-done(((bf16[1,64,512]{2,1,0:T(8,128)(2,1)}), bf16[1,1024,512]{2,1,0:T(8,128)(2,1)}) %all-gather.20.cloned.1.call-update) | async-done | bytes 1048592 | tf_op jit(solution)/shard_map/all_gather | solution.py:90
  111.6 3.0 convolution_convert_fusion.1
  114.6 0.8 fusion.157
  115.6 0.8 fusion.158
  116.7 37.1 %all-reduce.8.cloned.1.call-done = bf16[512,1024]{1,0:T(8,128)(2,1)} async-done(((bf16[512,1024]{1,0:T(8,128)(2,1)}), bf16[512,1024]{1,0:T(8,128)(2,1)}) %all-reduce.8.cloned.1.call-update) | async-done | bytes 1048592 | tf_op jit(solution)/shard_map/psum | solution.py:22
  153.8 1.7 fusion.56
  155.6 1.8 multiply_reduce_fusion.4
  158.0 8.5 %all-gather.22.cloned.1.call-done = bf16[1,1024,2048]{2,1,0:T(8,128)(2,1)} async-done(((bf16[1,64,2048]{2,1,0:T(8,128)(2,1)}), bf16[1,1024,2048]{2,1,0:T(8,128)(2,1)}) %all-gather.22.cloned.1.call-update) | async-done | bytes 4194320 | tf_op jit(solution)/shard_map/all_gather | solution.py:101
  166.5 51.6 %all-gather.24.cloned.1.call-done = bf16[1,1024,2048]{2,1,0:T(8,128)(2,1)} async-done(((bf16[1,64,2048]{2,1,0:T(8,128)(2,1)}), bf16[1,1024,2048]{2,1,0:T(8,128)(2,1)}) %all-gather.24.cloned.1.call-update) | async-done | bytes 4194320 | tf_op jit(solution)/shard_map/all_gather | solution.py:105
  218.2 16.7 %fusion.70 = bf16[512,1024]{1,0:T(8,128)(2,1)} fusion(bf16[1,1024,2048]{2,1,0:T(8,128)(2,1)} %all-gather.24.cloned.1.call-done, bf16[512,1024]{1,0:T(8,128)(2,1)S(1)} %add_convert_fusion.3, bf16[1,1024,2048]{2,1,0:T(8,128)(2,1)} %all-gather.22.cloned.1.call-done, f32[2048]{0:T(1024)S(1)} %bitcast.144), kind=kOutput, calls=%fused_computation.97 | convolution fusion | flops 4364697600 | bytes 10493952 | tf_op jit(solution)/shard_map/dot_general | solution.py:31
  235.0 0.7 all-gather.26.cloned.1.call-update
  235.7 0.7 all-gather.28.cloned.1.call-update
  236.5 37.3 %all-reduce.10.cloned.1.call-done = bf16[512,1024]{1,0:T(8,128)(2,1)} async-done(((bf16[512,1024]{1,0:T(8,128)(2,1)}), bf16[512,1024]{1,0:T(8,128)(2,1)}) %all-reduce.10.cloned.1.call-update) | async-done | bytes 1048592 | tf_op jit(solution)/shard_map/psum | solution.py:24
  273.7 1.8 fusion.57
  275.5 1.8 multiply_reduce_fusion.3
  277.9 3.7 all-gather.26.cloned.1.call-done
  281.6 3.7 fusion.64
  285.5 5.3 %fusion.166 = (f32[8,512]{1,0:T(8,128)S(1)}, f32[8,512,512]{1,2,0:T(8,128)}) fusion(pred[512]{0:T(512)(128)(4,1)S(1)} %iota_compare_fusion, bf16[512,8,64]{0,2,1:T(8,128)(2,1)S(1)} %bitcast.117, bf16[512,8,64]{0,2,1:T(8,128)(2,1)S(1)} %bitcast.116), kind=kOutput, calls=%fused_computation.203 | convolution fusion | flops 276824576 | bytes 9454080 | tf_op jit(solution)/shard_map/sub | solution.py:84
  290.8 4.2 fusion.80
  295.0 25.1 %all-gather.28.cloned.1.call-done = bf16[1,1024,512]{2,1,0:T(8,128)(2,1)} async-done(((bf16[1,64,512]{2,1,0:T(8,128)(2,1)}), bf16[1,1024,512]{2,1,0:T(8,128)(2,1)}) %all-gather.28.cloned.1.call-update) | async-done | bytes 1048592 | tf_op jit(solution)/shard_map/all_gather | solution.py:90
  320.1 2.9 convolution_convert_fusion
  324.6 37.8 %all-reduce.12.cloned.1.call-done = bf16[512,1024]{1,0:T(8,128)(2,1)} async-done(((bf16[512,1024]{1,0:T(8,128)(2,1)}), bf16[512,1024]{1,0:T(8,128)(2,1)}) %all-reduce.12.cloned.1.call-update) | async-done | bytes 1048592 | tf_op jit(solution)/shard_map/psum | solution.py:22
  362.3 1.8 fusion.58
  364.1 1.8 multiply_reduce_fusion.2
  366.0 0.6 add_convert_fusion.1
  366.6 8.4 %all-gather.30.cloned.1.call-done = bf16[1,1024,2048]{2,1,0:T(8,128)(2,1)} async-done(((bf16[1,64,2048]{2,1,0:T(8,128)(2,1)}), bf16[1,1024,2048]{2,1,0:T(8,128)(2,1)}) %all-gather.30.cloned.1.call-update) | async-done | bytes 4194320 | tf_op jit(solution)/shard_map/all_gather | solution.py:101
  375.0 50.9 %all-gather.32.cloned.1.call-done = bf16[1,1024,2048]{2,1,0:T(8,128)(2,1)} async-done(((bf16[1,64,2048]{2,1,0:T(8,128)(2,1)}), bf16[1,1024,2048]{2,1,0:T(8,128)(2,1)}) %all-gather.32.cloned.1.call-update) | async-done | bytes 4194320 | tf_op jit(solution)/shard_map/all_gather | solution.py:105
  425.9 16.9 %fusion.75 = bf16[512,1024]{1,0:T(8,128)(2,1)} fusion(bf16[1,1024,2048]{2,1,0:T(8,128)(2,1)} %all-gather.32.cloned.1.call-done, bf16[512,1024]{1,0:T(8,128)(2,1)S(1)} %add_convert_fusion.1, bf16[1,1024,2048]{2,1,0:T(8,128)(2,1)} %all-gather.30.cloned.1.call-done, f32[2048]{0:T(1024)S(1)} %bitcast.143), kind=kOutput, calls=%fused_computation.98 | convolution fusion | flops 4364697600 | bytes 10493952 | tf_op jit(solution)/shard_map/dot_general | solution.py:31
  442.9 38.8 %all-reduce.14.cloned.1.call-done = bf16[512,1024]{1,0:T(8,128)(2,1)} async-done(((bf16[512,1024]{1,0:T(8,128)(2,1)}), bf16[512,1024]{1,0:T(8,128)(2,1)}) %all-reduce.14.cloned.1.call-update) | async-done | bytes 1048592 | tf_op jit(solution)/shard_map/psum | solution.py:24
  481.7 1.8 fusion.59
  483.5 1.8 multiply_reduce_fusion.1
  485.3 0.9 multiply_reduce_fusion
  486.2 0.6 multiply_reduce_fusion.6
  487.5 21.5 %all-gather.8 = f32[16384]{0:T(1024)S(1)} all-gather(f32[1024]{0:T(1024)S(1)} %broadcast_multiply_fusion), channel_id=10, replica_groups=mesh['dp'=16,'tensor'=2] {'dp'}, dimensions={0}, use_global_device_ids=true | all-gather | bytes 69632 | tf_op jit(solution)/shard_map/all_gather | solution.py:124
  509.0 0.7 fusion.167
  509.8 0.8 constant_dynamic-slice_fusion
  (76 shorter events, 4.4 us)
Async XLA Ops:
  8.0 57.1 %all-reduce.6.cloned.1.call-start = ((), (), s32[]{:S(2)}) async-start(), calls=%async_computation | async-start | bytes 2097152 | tf_op jit(solution)/shard_map/psum | solution.py:57
  8.7 13.9 %copy-start.8 = (bf16[2,3,64,512]{3,2,1,0:T(8,128)(2,1)S(1)}, bf16[2,3,64,512]{3,2,1,0:T(8,128)(2,1)}, u32[]{:S(2)}) copy-start(bf16[2,3,64,512]{3,2,1,0:T(8,128)(2,1)} %param.16) | copy-start | bytes 1179652
  21.3 2.2 copy-start.9
  21.3 2.9 copy-start.12
  21.3 2.9 copy-start.13
  21.3 43.7 %copy-start = (bf16[512,1024]{1,0:T(8,128)(2,1)S(1)}, bf16[512,1024]{1,0:T(8,128)(2,1)}, u32[]{:S(2)}) copy-start(bf16[512,1024]{1,0:T(8,128)(2,1)} %param.15) | copy-start | bytes 3145732
  22.6 50.7 %all-gather.18.cloned.1.call-start = ((), (), s32[]{:S(2)}) async-start(), calls=%async_computation.5 | async-start | bytes 3342336 | tf_op jit(solution)/shard_map/all_gather | solution.py:70
  23.4 88.2 %all-gather.20.cloned.1.call-start = ((), (), s32[]{:S(2)}) async-start(), calls=%async_computation.6 | async-start | bytes 1114112 | tf_op jit(solution)/shard_map/all_gather | solution.py:90
  24.1 129.7 %all-reduce.8.cloned.1.call-start = ((), (), s32[]{:S(2)}) async-start(), calls=%async_computation.1 | async-start | bytes 2097152 | tf_op jit(solution)/shard_map/psum | solution.py:22
  65.1 3.4 copy-start.1
  86.6 28.0 %copy-start.6 = (bf16[2,64,2048]{2,1,0:T(8,128)(2,1)S(1)}, bf16[2,64,2048]{2,1,0:T(8,128)(2,1)}, u32[]{:S(2)}) copy-start(bf16[2,64,2048]{2,1,0:T(8,128)(2,1)} %param.18) | copy-start | bytes 1572868
  86.7 28.9 %copy-start.7 = (bf16[2,64,2048]{2,1,0:T(8,128)(2,1)S(1)}, bf16[2,64,2048]{2,1,0:T(8,128)(2,1)}, u32[]{:S(2)}) copy-start(bf16[2,64,2048]{2,1,0:T(8,128)(2,1)} %param.19) | copy-start | bytes 1572868
  86.7 30.0 %copy-start.10 = (f32[2,2,1024]{2,1,0:T(2,128)S(1)}, f32[2,2,1024]{2,1,0:T(2,128)}, u32[]{:S(2)}) copy-start(f32[2,2,1024]{2,1,0:T(2,128)} %param.21) | copy-start | bytes 49156
  86.7 30.0 %copy-start.11 = (f32[2,2048]{1,0:T(2,128)S(1)}, f32[2,2048]{1,0:T(2,128)}, u32[]{:S(2)}) copy-start(f32[2,2048]{1,0:T(2,128)} %param.20) | copy-start | bytes 49156
  114.6 52.0 %all-gather.22.cloned.1.call-start = ((), (), s32[]{:S(2)}) async-start(), calls=%async_computation.7 | async-start | bytes 4456448 | tf_op jit(solution)/shard_map/all_gather | solution.py:101
  115.5 102.7 %all-gather.24.cloned.1.call-start = ((), (), s32[]{:S(2)}) async-start(), calls=%async_computation.8 | async-start | bytes 4456448 | tf_op jit(solution)/shard_map/all_gather | solution.py:105
  116.4 157.3 %all-reduce.10.cloned.1.call-start = ((), (), s32[]{:S(2)}) async-start(), calls=%async_computation.2 | async-start | bytes 2097152 | tf_op jit(solution)/shard_map/psum | solution.py:24
  153.8 3.5 copy-start.2
  234.9 46.7 %all-gather.26.cloned.1.call-start = ((), (), s32[]{:S(2)}) async-start(), calls=%async_computation.9 | async-start | bytes 3342336 | tf_op jit(solution)/shard_map/all_gather | solution.py:70
  235.7 84.4 %all-gather.28.cloned.1.call-start = ((), (), s32[]{:S(2)}) async-start(), calls=%async_computation.10 | async-start | bytes 1114112 | tf_op jit(solution)/shard_map/all_gather | solution.py:90
  236.4 125.9 %all-reduce.12.cloned.1.call-start = ((), (), s32[]{:S(2)}) async-start(), calls=%async_computation.3 | async-start | bytes 2097152 | tf_op jit(solution)/shard_map/psum | solution.py:22
  273.7 3.6 copy-start.3
  323.1 52.0 %all-gather.30.cloned.1.call-start = ((), (), s32[]{:S(2)}) async-start(), calls=%async_computation.11 | async-start | bytes 4456448 | tf_op jit(solution)/shard_map/all_gather | solution.py:101
  323.7 102.3 %all-gather.32.cloned.1.call-start = ((), (), s32[]{:S(2)}) async-start(), calls=%async_computation.12 | async-start | bytes 4456448 | tf_op jit(solution)/shard_map/all_gather | solution.py:105
  324.2 157.4 %all-reduce.14.cloned.1.call-start = ((), (), s32[]{:S(2)}) async-start(), calls=%async_computation.4 | async-start | bytes 2097152 | tf_op jit(solution)/shard_map/psum | solution.py:24
  362.3 3.6 copy-start.4
  481.7 3.6 copy-start.5
Sparse Core Ops, SparseCore 0:
  22.7 42.3 all-reduce.5
  114.7 39.0 all-reduce.7
  235.0 38.6 all-reduce.9
  323.2 39.1 all-reduce.11
  443.0 38.6 all-reduce.13
Sparse Core Ops, SparseCore 1:
  25.8 47.4 all-gather.17
  75.3 36.2 all-gather.19
  117.2 49.2 all-gather.21
  169.3 48.8 all-gather.23
  237.9 43.6 all-gather.25
  283.8 36.2 all-gather.27
  325.7 49.2 all-gather.29
  377.1 48.8 all-gather.31
where the time goes:
time: 526 us; the launch traced here: 518 us
  waiting for transfers between devices  371 us (71%)
  matrix products  66.8 us (13%)
  other arithmetic  23.5 us (4%)
  blocking collectives  21.5 us (4%)
  between operations  17.5 us (3%)
  local copies, waits for them, and re-layouts  16.8 us (3%)
    psum x4, waiting for transfers between devices, settle(): summed = lax.psum(partial_value, 'tensor').astype(jnp.float32)  151 us
    all_gather x2, waiting for transfers between devices, per_device(): lax.all_gather(w_down[layer], 'dp', axis=0, tiled=True)  103 us
    all_gather x2, waiting for transfers between devices, per_device(): lax.all_gather(w_out[layer], 'dp', axis=0, tiled=True)  50 us
    psum x1, waiting for transfers between devices, per_device(): embedded = lax.psum(picked, 'tensor').astype(jnp.float32)  40.1 us
    dot_general x4, matrix products, project_back(): lax.dot_general(left, weight, (((1,), (1,)), ((), ())), preferred_element...  39.5 us
    all_gather x1, blocking collectives, per_device(): every_unit = lax.all_gather(unit, 'dp', axis=0, tiled=True)  21.5 us
    all_gather x2, waiting for transfers between devices, per_device(): lax.all_gather(w_up[layer], 'dp', axis=0, tiled=True)  17 us
    gather x1, local copies, waits for them, and re-layouts, per_device(): jnp.take(word_table, jnp.clip(local_ids, 0, vocab_rows - 1), axis=0)  12.5 us
  transfers between devices with their start and end apart: 13, of which 13 were waited for; matrix products, arithmetic and copies ran while one was open for 9% of the time, Pallas kernels for 0%

commit v1 on v0

--- a/solution.py
+++ b/solution.py
@@ -54,7 +54,7 @@
     inside = (local_ids >= 0) & (local_ids < vocab_rows)
     picked = jnp.take(word_table, jnp.clip(local_ids, 0, vocab_rows - 1), axis=0)
     picked = jnp.where(inside[:, None], picked, jnp.zeros_like(picked))
-    embedded = lax.psum(picked, "tensor").astype(jnp.float32)
+    embedded = jnp.sum(lax.all_gather(picked, "tensor"), axis=0).astype(jnp.float32)
     embedded = embedded.reshape(passage_count, BLOCK, D) + pos_table.astype(jnp.float32)[None]
     hidden = layer_norm(
         embedded.reshape(passage_count * BLOCK, D), norm_gain[0], norm_bias[0]

time: 526 us -> 677 us (1.29)
  waiting for transfers between devices: 371 us -> 524 us
    all_gather x2, waiting for transfers between devices: 7.92 us -> 88.2 us  [per_device(): lax.all_gather(w_qkv[layer], 'dp', axis=1, tiled=True)]
    all_gather x2, waiting for transfers between devices: 17 us -> 96.6 us  [per_device(): lax.all_gather(w_up[layer], 'dp', axis=0, tiled=True)]
    psum x1 -> x0, waiting for transfers between devices: 40.1 us -> none  [per_device(): embedded = lax.psum(picked, 'tensor').astype(jnp.float32)]
    all_gather x0 -> x1, waiting for transfers between devices: none -> 33.1 us  [per_device(): lax.all_gather(picked, 'tensor')]
  transfers between devices with their start and end apart: 13 -> 13, of which waited for: 13 -> 13; matrix products, arithmetic and copies ran while one was open for 9% -> 7% of each run, Pallas kernels for 0% -> 0%
where the time goes in v1:
time: 677 us; the launch traced here: 669 us
  waiting for transfers between devices  524 us (77%)
  matrix products  66.8 us (10%)
  other arithmetic  23.2 us (3%)
  blocking collectives  21.5 us (3%)
  local copies, waits for them, and re-layouts  16.8 us (2%)
  between operations  16.1 us (2%)
    psum x4, waiting for transfers between devices, settle(): summed = lax.psum(partial_value, 'tensor').astype(jnp.float32)  151 us
    all_gather x2, waiting for transfers between devices, per_device(): lax.all_gather(w_down[layer], 'dp', axis=0, tiled=True)  102 us
    all_gather x2, waiting for transfers between devices, per_device(): lax.all_gather(w_up[layer], 'dp', axis=0, tiled=True)  96.6 us
    all_gather x2, waiting for transfers between devices, per_device(): lax.all_gather(w_qkv[layer], 'dp', axis=1, tiled=True)  88.2 us
    all_gather x2, waiting for transfers between devices, per_device(): lax.all_gather(w_out[layer], 'dp', axis=0, tiled=True)  50.1 us
    dot_general x4, matrix products, project_back(): lax.dot_general(left, weight, (((1,), (1,)), ((), ())), preferred_element...  39.5 us
    all_gather x1, waiting for transfers between devices, per_device(): lax.all_gather(picked, 'tensor')  33.1 us
    all_gather x1, blocking collectives, per_device(): every_unit = lax.all_gather(unit, 'dp', axis=0, tiled=True)  21.5 us
  transfers between devices with their start and end apart: 13, of which 13 were waited for; matrix products, arithmetic and copies ran while one was open for 7% of the time, Pallas kernels for 0%

profile of v1, /device:TPU:0, one launch (start us, length us, event | category | flops | bytes accessed | tf_op | source)
XLA Modules:
  0.0 669.2 jit_solution(12864401605700107418)
XLA Ops:
  7.2 0.7 compare_and_fusion
  7.9 12.5 %gather_fusion = bf16[512,1024]{1,0:T(8,128)(2,1)S(1)} fusion(bf16[15360,1024]{1,0:T(8,128)(2,1)} %param.14, s32[1024]{0:T(1024)S(1)} %pad_clamp_fusion), kind=kCustom, calls=%fused_computation | custom fusion | bytes 2099200 | tf_op jit(solution)/shard_map/jit(_take)/gather | solution.py:55
  20.5 1.2 fusion.86
  21.8 0.8 fusion.160
  22.6 0.7 fusion.161
  24.1 33.1 %all-gather.19.cloned.1.call-done = bf16[2,512,1024]{2,1,0:T(8,128)(2,1)} async-done(((bf16[1,512,1024]{2,1,0:T(8,128)(2,1)}), bf16[2,512,1024]{2,1,0:T(8,128)(2,1)}) %all-gather.19.cloned.1.call-update) | async-done | bytes 2097168 | tf_op jit(solution)/shard_map/all_gather | solution.py:57
  57.2 2.2 reduce_sum.138
  60.8 44.7 %all-gather.21.cloned.1.call-done = bf16[1,3,1024,512]{3,2,1,0:T(8,128)(2,1)} async-done(((bf16[1,3,64,512]{3,2,1,0:T(8,128)(2,1)}), bf16[1,3,1024,512]{3,2,1,0:T(8,128)(2,1)}) %all-gather.21.cloned.1.call-update) | async-done | bytes 3145744 | tf_op jit(solution)/shard_map/all_gather | solution.py:70
  105.5 3.7 fusion.67
  109.4 5.3 fusion.166
  114.7 4.2 fusion.81
  119.0 25.0 %all-gather.23.cloned.1.call-done = bf16[1,1024,512]{2,1,0:T(8,128)(2,1)} async-done(((bf16[1,64,512]{2,1,0:T(8,128)(2,1)}), bf16[1,1024,512]{2,1,0:T(8,128)(2,1)}) %all-gather.23.cloned.1.call-update) | async-done | bytes 1048592 | tf_op jit(solution)/shard_map/all_gather | solution.py:90
  144.0 3.0 convolution_convert_fusion.1
  147.0 0.9 fusion.158
  148.0 0.8 fusion.159
  149.1 37.1 %all-reduce.5.cloned.1.call-done = bf16[512,1024]{1,0:T(8,128)(2,1)} async-done(((bf16[512,1024]{1,0:T(8,128)(2,1)}), bf16[512,1024]{1,0:T(8,128)(2,1)}) %all-reduce.5.cloned.1.call-update) | async-done | bytes 1048592 | tf_op jit(solution)/shard_map/psum | solution.py:22
  186.2 1.7 fusion.56
  188.0 1.8 multiply_reduce_fusion.4
  190.4 48.3 %all-gather.25.cloned.1.call-done = bf16[1,1024,2048]{2,1,0:T(8,128)(2,1)} async-done(((bf16[1,64,2048]{2,1,0:T(8,128)(2,1)}), bf16[1,1024,2048]{2,1,0:T(8,128)(2,1)}) %all-gather.25.cloned.1.call-update) | async-done | bytes 4194320 | tf_op jit(solution)/shard_map/all_gather | solution.py:101
  238.6 51.5 %all-gather.27.cloned.1.call-done = bf16[1,1024,2048]{2,1,0:T(8,128)(2,1)} async-done(((bf16[1,64,2048]{2,1,0:T(8,128)(2,1)}), bf16[1,1024,2048]{2,1,0:T(8,128)(2,1)}) %all-gather.27.cloned.1.call-update) | async-done | bytes 4194320 | tf_op jit(solution)/shard_map/all_gather | solution.py:105
  290.2 16.7 %fusion.70 = bf16[512,1024]{1,0:T(8,128)(2,1)} fusion(bf16[1,1024,2048]{2,1,0:T(8,128)(2,1)} %all-gather.27.cloned.1.call-done, bf16[512,1024]{1,0:T(8,128)(2,1)S(1)} %add_convert_fusion.3, bf16[1,1024,2048]{2,1,0:T(8,128)(2,1)} %all-gather.25.cloned.1.call-done, f32[2048]{0:T(1024)S(1)} %bitcast.148), kind=kOutput, calls=%fused_computation.97 | convolution fusion | flops 4364697600 | bytes 10493952 | tf_op jit(solution)/shard_map/dot_general | solution.py:31
  307.0 0.7 all-gather.29.cloned.1.call-update
  307.7 0.7 all-gather.31.cloned.1.call-update
  308.5 37.3 %all-reduce.7.cloned.1.call-done = bf16[512,1024]{1,0:T(8,128)(2,1)} async-done(((bf16[512,1024]{1,0:T(8,128)(2,1)}), bf16[512,1024]{1,0:T(8,128)(2,1)}) %all-reduce.7.cloned.1.call-update) | async-done | bytes 1048592 | tf_op jit(solution)/shard_map/psum | solution.py:24
  345.7 1.7 fusion.57
  347.5 1.8 multiply_reduce_fusion.3
  349.9 43.5 %all-gather.29.cloned.1.call-done = bf16[1,3,1024,512]{3,2,1,0:T(8,128)(2,1)} async-done(((bf16[1,3,64,512]{3,2,1,0:T(8,128)(2,1)}), bf16[1,3,1024,512]{3,2,1,0:T(8,128)(2,1)}) %all-gather.29.cloned.1.call-update) | async-done | bytes 3145744 | tf_op jit(solution)/shard_map/all_gather | solution.py:70
  393.4 3.7 fusion.64
  397.3 5.3 fusion.167
  402.6 4.2 fusion.80
  406.8 25.1 %all-gather.31.cloned.1.call-done = bf16[1,1024,512]{2,1,0:T(8,128)(2,1)} async-done(((bf16[1,64,512]{2,1,0:T(8,128)(2,1)}), bf16[1,1024,512]{2,1,0:T(8,128)(2,1)}) %all-gather.31.cloned.1.call-update) | async-done | bytes 1048592 | tf_op jit(solution)/shard_map/all_gather | solution.py:90
  431.9 2.9 convolution_convert_fusion
  434.9 0.7 all-gather.33.cloned.1.call-update
  436.5 37.6 %all-reduce.9.cloned.1.call-done = bf16[512,1024]{1,0:T(8,128)(2,1)} async-done(((bf16[512,1024]{1,0:T(8,128)(2,1)}), bf16[512,1024]{1,0:T(8,128)(2,1)}) %all-reduce.9.cloned.1.call-update) | async-done | bytes 1048592 | tf_op jit(solution)/shard_map/psum | solution.py:22
  474.1 1.8 fusion.58
  475.9 1.8 multiply_reduce_fusion.2
  477.7 0.6 add_convert_fusion.1
  478.3 48.3 %all-gather.33.cloned.1.call-done = bf16[1,1024,2048]{2,1,0:T(8,128)(2,1)} async-done(((bf16[1,64,2048]{2,1,0:T(8,128)(2,1)}), bf16[1,1024,2048]{2,1,0:T(8,128)(2,1)}) %all-gather.33.cloned.1.call-update) | async-done | bytes 4194320 | tf_op jit(solution)/shard_map/all_gather | solution.py:101
  526.7 51.0 %all-gather.35.cloned.1.call-done = bf16[1,1024,2048]{2,1,0:T(8,128)(2,1)} async-done(((bf16[1,64,2048]{2,1,0:T(8,128)(2,1)}), bf16[1,1024,2048]{2,1,0:T(8,128)(2,1)}) %all-gather.35.cloned.1.call-update) | async-done | bytes 4194320 | tf_op jit(solution)/shard_map/all_gather | solution.py:105
  577.6 16.9 %fusion.75 = bf16[512,1024]{1,0:T(8,128)(2,1)} fusion(bf16[1,1024,2048]{2,1,0:T(8,128)(2,1)} %all-gather.35.cloned.1.call-done, bf16[512,1024]{1,0:T(8,128)(2,1)S(1)} %add_convert_fusion.1, bf16[1,1024,2048]{2,1,0:T(8,128)(2,1)} %all-gather.33.cloned.1.call-done, f32[2048]{0:T(1024)S(1)} %bitcast.147), kind=kOutput, calls=%fused_computation.98 | convolution fusion | flops 4364697600 | bytes 10493952 | tf_op jit(solution)/shard_map/dot_general | solution.py:31
  594.6 38.8 %all-reduce.11.cloned.1.call-done = bf16[512,1024]{1,0:T(8,128)(2,1)} async-done(((bf16[512,1024]{1,0:T(8,128)(2,1)}), bf16[512,1024]{1,0:T(8,128)(2,1)}) %all-reduce.11.cloned.1.call-update) | async-done | bytes 1048592 | tf_op jit(solution)/shard_map/psum | solution.py:24
  633.3 1.8 fusion.59
  635.1 1.8 multiply_reduce_fusion.1
  637.0 0.9 multiply_reduce_fusion
  637.8 0.6 multiply_reduce_fusion.6
  639.2 21.5 %all-gather.8 = f32[16384]{0:T(1024)S(1)} all-gather(f32[1024]{0:T(1024)S(1)} %broadcast_multiply_fusion), channel_id=10, replica_groups=mesh['dp'=16,'tensor'=2] {'dp'}, dimensions={0}, use_global_device_ids=true | all-gather | bytes 69632 | tf_op jit(solution)/shard_map/all_gather | solution.py:124
  660.7 0.7 fusion.168
  661.4 0.8 constant_dynamic-slice_fusion
  (75 shorter events, 4.7 us)
Async XLA Ops:
  7.2 50.1 %all-gather.19.cloned.1.call-start = ((), (), s32[]{:S(2)}) async-start(), calls=%async_computation | async-start | bytes 3145728 | tf_op jit(solution)/shard_map/all_gather | solution.py:57
  7.9 13.9 %copy-start.7 = (bf16[2,3,64,512]{3,2,1,0:T(8,128)(2,1)S(1)}, bf16[2,3,64,512]{3,2,1,0:T(8,128)(2,1)}, u32[]{:S(2)}) copy-start(bf16[2,3,64,512]{3,2,1,0:T(8,128)(2,1)} %param.16) | copy-start | bytes 1179652
  20.4 2.2 copy-start.8
  20.5 2.9 copy-start.11
  20.5 2.9 copy-start.12
  20.5 38.9 %copy-start = (bf16[512,1024]{1,0:T(8,128)(2,1)S(1)}, bf16[512,1024]{1,0:T(8,128)(2,1)}, u32[]{:S(2)}) copy-start(bf16[512,1024]{1,0:T(8,128)(2,1)} %param.15) | copy-start | bytes 3145732
  21.7 83.8 %all-gather.21.cloned.1.call-start = ((), (), s32[]{:S(2)}) async-start(), calls=%async_computation.5 | async-start | bytes 3342336 | tf_op jit(solution)/shard_map/all_gather | solution.py:70
  22.6 121.4 %all-gather.23.cloned.1.call-start = ((), (), s32[]{:S(2)}) async-start(), calls=%async_computation.6 | async-start | bytes 1114112 | tf_op jit(solution)/shard_map/all_gather | solution.py:90
  23.3 162.9 %all-reduce.5.cloned.1.call-start = ((), (), s32[]{:S(2)}) async-start(), calls=%async_computation.1 | async-start | bytes 2097152 | tf_op jit(solution)/shard_map/psum | solution.py:22
  118.9 28.1 %copy-start.5 = (bf16[2,64,2048]{2,1,0:T(8,128)(2,1)S(1)}, bf16[2,64,2048]{2,1,0:T(8,128)(2,1)}, u32[]{:S(2)}) copy-start(bf16[2,64,2048]{2,1,0:T(8,128)(2,1)} %param.18) | copy-start | bytes 1572868
  119.0 29.0 %copy-start.6 = (bf16[2,64,2048]{2,1,0:T(8,128)(2,1)S(1)}, bf16[2,64,2048]{2,1,0:T(8,128)(2,1)}, u32[]{:S(2)}) copy-start(bf16[2,64,2048]{2,1,0:T(8,128)(2,1)} %param.19) | copy-start | bytes 1572868
  119.0 30.1 %copy-start.9 = (f32[2,2,1024]{2,1,0:T(2,128)S(1)}, f32[2,2,1024]{2,1,0:T(2,128)}, u32[]{:S(2)}) copy-start(f32[2,2,1024]{2,1,0:T(2,128)} %param.21) | copy-start | bytes 49156
  119.0 30.1 %copy-start.10 = (f32[2,2048]{1,0:T(2,128)S(1)}, f32[2,2048]{1,0:T(2,128)}, u32[]{:S(2)}) copy-start(f32[2,2048]{1,0:T(2,128)} %param.20) | copy-start | bytes 49156
  147.0 91.6 %all-gather.25.cloned.1.call-start = ((), (), s32[]{:S(2)}) async-start(), calls=%async_computation.7 | async-start | bytes 4456448 | tf_op jit(solution)/shard_map/all_gather | solution.py:101
  147.9 142.2 %all-gather.27.cloned.1.call-start = ((), (), s32[]{:S(2)}) async-start(), calls=%async_computation.8 | async-start | bytes 4456448 | tf_op jit(solution)/shard_map/all_gather | solution.py:105
  148.8 196.9 %all-reduce.7.cloned.1.call-start = ((), (), s32[]{:S(2)}) async-start(), calls=%async_computation.2 | async-start | bytes 2097152 | tf_op jit(solution)/shard_map/psum | solution.py:24
  186.2 3.5 copy-start.1
  306.9 86.5 %all-gather.29.cloned.1.call-start = ((), (), s32[]{:S(2)}) async-start(), calls=%async_computation.9 | async-start | bytes 3342336 | tf_op jit(solution)/shard_map/all_gather | solution.py:70
  307.7 124.2 %all-gather.31.cloned.1.call-start = ((), (), s32[]{:S(2)}) async-start(), calls=%async_computation.10 | async-start | bytes 1114112 | tf_op jit(solution)/shard_map/all_gather | solution.py:90
  308.4 165.7 %all-reduce.9.cloned.1.call-start = ((), (), s32[]{:S(2)}) async-start(), calls=%async_computation.3 | async-start | bytes 2097152 | tf_op jit(solution)/shard_map/psum | solution.py:22
  345.7 3.6 copy-start.2
  434.9 91.8 %all-gather.33.cloned.1.call-start = ((), (), s32[]{:S(2)}) async-start(), calls=%async_computation.11 | async-start | bytes 4456448 | tf_op jit(solution)/shard_map/all_gather | solution.py:101
  435.6 142.0 %all-gather.35.cloned.1.call-start = ((), (), s32[]{:S(2)}) async-start(), calls=%async_computation.12 | async-start | bytes 4456448 | tf_op jit(solution)/shard_map/all_gather | solution.py:105
  436.2 197.2 %all-reduce.11.cloned.1.call-start = ((), (), s32[]{:S(2)}) async-start(), calls=%async_computation.4 | async-start | bytes 2097152 | tf_op jit(solution)/shard_map/psum | solution.py:24
  474.1 3.6 copy-start.3
  633.3 3.6 copy-start.4
Sparse Core Ops, SparseCore 0:
  21.9 35.3 all-gather.18
  60.0 45.4 all-gather.20
  107.7 36.2 all-gather.22
  147.1 39.0 all-reduce.4
  188.2 50.3 all-gather.24
  241.2 48.8 all-gather.26
  307.0 38.6 all-reduce.6
  347.9 45.4 all-gather.28
  395.6 36.2 all-gather.30
  435.0 39.0 all-reduce.8
  476.2 50.3 all-gather.32
  528.7 48.8 all-gather.34
  594.7 38.6 all-reduce.10
